TPU v7x, 32 devices: a whole 2x2x4 slice. The times are simulated.
32 devices in a mesh: shard: 8 (over y, x, core), tensor: 4 (over z).
Axes of the slice: x: 2, y: 2, z: 4, core: 2. Of those that a mesh axis runs over, the one named last changes fastest.
Arguments:
- tokens: bfloat16 [16384, 2048], P('shard'), may hold values from -40 to 40
- ln1_gain: bfloat16 [2048], P('shard'), may hold values from 0.25 to 1.75
- ln1_bias: bfloat16 [2048], P('shard'), may hold values from -3 to 3
- qkv_weight: bfloat16 [2048, 8, 3, 256], P('shard', 'tensor'), may hold values from -2 to 2
- qkv_bias: bfloat16 [8, 3, 256], P('tensor'), may hold values from -3 to 3
- out_weight: bfloat16 [2048, 8, 256], P('shard', 'tensor'), may hold values from -0.5 to 0.5
- out_bias: bfloat16 [2048], P('shard'), may hold values from -3 to 3
- ln2_gain: bfloat16 [2048], P('shard'), may hold values from 0.25 to 1.75
- ln2_bias: bfloat16 [2048], P('shard'), may hold values from -3 to 3
- fc1_weight: bfloat16 [2048, 8192], P('shard', 'tensor'), may hold values from -0.125 to 0.125
- fc1_bias: bfloat16 [8192], P('tensor'), may hold values from -3 to 3
- fc2_weight: bfloat16 [2048, 8192], P('shard', 'tensor'), may hold values from -0.0625 to 0.0625
- fc2_bias: bfloat16 [2048], P('shard'), may hold values from -3 to 3
- cotangent: bfloat16 [16384, 2048], P('shard'), may hold values from -6 to 6
Outputs:
- block_out: bfloat16 [16384, 2048], P('shard')
- grad_tokens: float32 [16384, 2048], P('shard')
- grad_ln1_gain: float32 [2048], P('shard')
- grad_ln1_bias: float32 [2048], P('shard')
- grad_qkv_weight: float32 [2048, 8, 3, 256], P('shard', 'tensor')
- grad_qkv_bias: float32 [8, 3, 256], P('tensor')
- grad_out_weight: float32 [2048, 8, 256], P('shard', 'tensor')
- grad_out_bias: float32 [2048], P('shard')
- grad_ln2_gain: float32 [2048], P('shard')
- grad_ln2_bias: float32 [2048], P('shard')
- grad_fc1_weight: float32 [2048, 8192], P('shard', 'tensor')
- grad_fc1_bias: float32 [8192], P('tensor')
- grad_fc2_weight: float32 [2048, 8192], P('shard', 'tensor')
- grad_fc2_bias: float32 [2048], P('shard')
All inputs are finite; a program needn't handle non-finite values.
Results may differ from a plain program's by a relative error of at most 0.017.
Values may be sent and summed in bfloat16 or wider, within the bound.
A program may use at most 320 MiB of HBM per device.

v0:
```python
import math
import jax
import jax.numpy as jnp
from jax import lax
from jax.sharding import PartitionSpec as P

ROT = 64
SEQ = 256
MICRO = 2
NORM_EPS = 1e-05
ROOT_HALF = 0.7071067811865476
INV_ROOT_TWO_PI = 0.3989422804014327


def as_sent(shard):

    def short(part):
        return part.astype(jnp.bfloat16) if part.dtype == jnp.float32 else part

    return jax.tree.map(short, shard)


def normalize(residual):
    row_mean = jnp.mean(residual, axis=-1, keepdims=True)
    centered = residual - row_mean
    row_var = jnp.mean(centered * centered, axis=-1, keepdims=True)
    inv_std = lax.rsqrt(row_var + NORM_EPS)
    return (centered * inv_std, inv_std)


def norm_backward(grad_normed, gain_wide, normalized, inv_std):
    scaled_grad = grad_normed * gain_wide
    return inv_std * (
        scaled_grad
        - jnp.mean(scaled_grad, axis=-1, keepdims=True)
        - normalized * jnp.mean(scaled_grad * normalized, axis=-1, keepdims=True)
    )


def rotary_tables(length, rot_dims):
    half_dims = rot_dims // 2
    frequency = jnp.power(10000.0, -2.0 * jnp.arange(half_dims, dtype=jnp.float32) / rot_dims)
    angles = jnp.arange(length, dtype=jnp.float32)[:, None] * frequency[None, :]
    return (jnp.cos(angles), jnp.sin(angles))


def rotate(field, cos_tab, sin_tab, rot_dims):
    half_dims = rot_dims // 2
    lower_half = field[..., :half_dims]
    upper_half = field[..., half_dims:rot_dims]
    cos_wide = cos_tab[None, :, None, :]
    sin_wide = sin_tab[None, :, None, :]
    return jnp.concatenate(
        [
            lower_half * cos_wide - upper_half * sin_wide,
            upper_half * cos_wide + lower_half * sin_wide,
            field[..., rot_dims:],
        ],
        axis=-1,
    )


def rotate_back(grad_field, cos_tab, sin_tab, rot_dims):
    half_dims = rot_dims // 2
    lower_half = grad_field[..., :half_dims]
    upper_half = grad_field[..., half_dims:rot_dims]
    cos_wide = cos_tab[None, :, None, :]
    sin_wide = sin_tab[None, :, None, :]
    return jnp.concatenate(
        [
            lower_half * cos_wide + upper_half * sin_wide,
            upper_half * cos_wide - lower_half * sin_wide,
            grad_field[..., rot_dims:],
        ],
        axis=-1,
    )


def gelu_exact(pre_act):
    return 0.5 * pre_act * (1.0 + lax.erf(pre_act * ROOT_HALF))


def gelu_slope(pre_act):
    return (
        0.5 * (1.0 + lax.erf(pre_act * ROOT_HALF))
        + pre_act * jnp.exp(-0.5 * pre_act * pre_act) * INV_ROOT_TWO_PI
    )


def causal_scores(queries, key_rows, score_scale):
    length = queries.shape[1]
    scores = (
        jnp.einsum("nqhc,nkhc->nhqk", queries, key_rows, preferred_element_type=jnp.float32)
        * score_scale
    )
    causal = jnp.arange(length)[:, None] >= jnp.arange(length)[None, :]
    return jnp.where(causal[None, None], scores, -1e30)


def add_pairs(older, newer):
    return tuple((first_term + second_term for first_term, second_term in zip(older, newer)))


def forward_pass(x_block, weights, qkv_shift, fc1_shift, cos_tab, sin_tab):
    (
        qkv_full,
        out_full,
        fc1_full,
        fc2_full,
        gain_one,
        bias_one,
        gain_two,
        bias_two,
        out_shift,
        fc2_shift,
    ) = weights
    row_count = x_block.shape[0]
    seq_count = row_count // SEQ
    head_count = qkv_full.shape[1]
    head_dim = qkv_full.shape[3]
    residual = x_block.astype(jnp.float32)
    normalized, inv_std = normalize(residual)
    normed_one = (normalized * gain_one.astype(jnp.float32) + bias_one.astype(jnp.float32)).astype(
        jnp.bfloat16
    )
    normed_two = (normalized * gain_two.astype(jnp.float32) + bias_two.astype(jnp.float32)).astype(
        jnp.bfloat16
    )
    qkv = jnp.einsum("md,dhkc->mhkc", normed_one, qkv_full, preferred_element_type=jnp.float32)
    qkv = qkv + qkv_shift.astype(jnp.float32)
    fields = qkv.reshape(seq_count, SEQ, head_count, 3, head_dim)
    queries = rotate(fields[:, :, :, 0], cos_tab, sin_tab, ROT).astype(jnp.bfloat16)
    key_rows = rotate(fields[:, :, :, 1], cos_tab, sin_tab, ROT).astype(jnp.bfloat16)
    values = fields[:, :, :, 2].astype(jnp.bfloat16)
    score_scale = 1.0 / math.sqrt(head_dim)
    scores = causal_scores(queries, key_rows, score_scale)
    row_top = jnp.max(scores, axis=-1, keepdims=True)
    log_total = row_top + jnp.log(jnp.sum(jnp.exp(scores - row_top), axis=-1, keepdims=True))
    attn_probs = jnp.exp(scores - log_total).astype(jnp.bfloat16)
    attn_out = jnp.einsum("nhqk,nkhc->nqhc", attn_probs, values, preferred_element_type=jnp.float32)
    attn_out = attn_out.astype(jnp.bfloat16).reshape(row_count, head_count, head_dim)
    pre_act = jnp.dot(normed_two, fc1_full, preferred_element_type=jnp.float32) + fc1_shift.astype(
        jnp.float32
    )
    hidden = gelu_exact(pre_act).astype(jnp.bfloat16)
    partial_value = jnp.einsum(
        "mhc,dhc->md", attn_out, out_full, preferred_element_type=jnp.float32
    )
    partial_value = partial_value + jnp.einsum(
        "mf,df->md", hidden, fc2_full, preferred_element_type=jnp.float32
    )
    saved = (
        residual,
        normalized,
        inv_std,
        normed_one,
        normed_two,
        queries,
        key_rows,
        values,
        log_total,
        attn_out,
        pre_act,
        hidden,
    )
    return (partial_value, saved)


def backward_pass(grad_block, saved, weights, cos_tab, sin_tab):
    (
        qkv_full,
        out_full,
        fc1_full,
        fc2_full,
        gain_one,
        bias_one,
        gain_two,
        bias_two,
        out_shift,
        fc2_shift,
    ) = weights
    (
        residual,
        normalized,
        inv_std,
        normed_one,
        normed_two,
        queries,
        key_rows,
        values,
        log_total,
        attn_out,
        pre_act,
        hidden,
    ) = saved
    row_count = grad_block.shape[0]
    seq_count = row_count // SEQ
    head_count = qkv_full.shape[1]
    head_dim = qkv_full.shape[3]
    score_scale = 1.0 / math.sqrt(head_dim)
    grad_wide = grad_block.astype(jnp.float32)
    shift_grad = jnp.sum(grad_wide, axis=0)
    grad_out_w = jnp.einsum("md,mhc->dhc", grad_block, attn_out, preferred_element_type=jnp.float32)
    grad_fc2_w = jnp.einsum("md,mf->df", grad_block, hidden, preferred_element_type=jnp.float32)
    d_attn = jnp.einsum("md,dhc->mhc", grad_block, out_full, preferred_element_type=jnp.float32)
    d_attn = d_attn.astype(jnp.bfloat16).reshape(seq_count, SEQ, head_count, head_dim)
    d_pre = jnp.dot(grad_block, fc2_full, preferred_element_type=jnp.float32) * gelu_slope(pre_act)
    fc1_shift_grad = jnp.sum(d_pre, axis=0)
    d_pre_b = d_pre.astype(jnp.bfloat16)
    grad_fc1_w = jnp.einsum("md,mf->df", normed_two, d_pre_b, preferred_element_type=jnp.float32)
    d_two = jnp.einsum("mf,df->md", d_pre_b, fc1_full, preferred_element_type=jnp.float32)
    probs_again = jnp.exp(causal_scores(queries, key_rows, score_scale) - log_total)
    d_values = jnp.einsum(
        "nhqk,nqhc->nkhc",
        probs_again.astype(jnp.bfloat16),
        d_attn,
        preferred_element_type=jnp.float32,
    )
    d_probs = jnp.einsum("nqhc,nkhc->nhqk", d_attn, values, preferred_element_type=jnp.float32)
    row_delta = jnp.sum(probs_again * d_probs, axis=-1, keepdims=True)
    d_scores = (probs_again * (d_probs - row_delta) * score_scale).astype(jnp.bfloat16)
    d_queries = rotate_back(
        jnp.einsum("nhqk,nkhc->nqhc", d_scores, key_rows, preferred_element_type=jnp.float32),
        cos_tab,
        sin_tab,
        ROT,
    )
    d_keys = rotate_back(
        jnp.einsum("nhqk,nqhc->nkhc", d_scores, queries, preferred_element_type=jnp.float32),
        cos_tab,
        sin_tab,
        ROT,
    )
    d_qkv = jnp.stack([d_queries, d_keys, d_values], axis=3).reshape(
        row_count, head_count, 3, head_dim
    )
    qkv_shift_grad = jnp.sum(d_qkv, axis=0)
    d_qkv_b = d_qkv.astype(jnp.bfloat16)
    grad_qkv_w = jnp.einsum(
        "md,mhkc->dhkc", normed_one, d_qkv_b, preferred_element_type=jnp.float32
    )
    d_one = jnp.einsum("mhkc,dhkc->md", d_qkv_b, qkv_full, preferred_element_type=jnp.float32)
    d_input = norm_backward(
        d_one, gain_one.astype(jnp.float32), normalized, inv_std
    ) + norm_backward(d_two, gain_two.astype(jnp.float32), normalized, inv_std)
    norm_terms = jnp.stack(
        [
            jnp.sum(d_one * normalized, axis=0),
            jnp.sum(d_one, axis=0),
            jnp.sum(d_two * normalized, axis=0),
            jnp.sum(d_two, axis=0),
        ]
    )
    matrix_grads = (grad_qkv_w, grad_out_w, grad_fc1_w, grad_fc2_w)
    return (d_input, norm_terms, matrix_grads, shift_grad, qkv_shift_grad, fc1_shift_grad)


def per_device(
    tokens,
    ln1_gain,
    ln1_bias,
    qkv_weight,
    qkv_bias,
    out_weight,
    out_bias,
    ln2_gain,
    ln2_bias,
    fc1_weight,
    fc1_bias,
    fc2_weight,
    fc2_bias,
    cotangent,
):
    own_shards = (
        qkv_weight,
        out_weight,
        fc1_weight,
        fc2_weight,
        ln1_gain,
        ln1_bias,
        ln2_gain,
        ln2_bias,
        out_bias,
        fc2_bias,
    )
    micro_rows = tokens.shape[0] // MICRO
    cos_tab, sin_tab = rotary_tables(SEQ, ROT)
    outputs = []
    grad_outputs = []
    grad_accum = None
    qkv_shift_acc = jnp.zeros(qkv_bias.shape, jnp.float32)
    fc1_shift_acc = jnp.zeros(fc1_bias.shape, jnp.float32)
    for micro_index in range(MICRO):
        x_block = tokens[micro_index * micro_rows : (micro_index + 1) * micro_rows]
        grad_block = cotangent[micro_index * micro_rows : (micro_index + 1) * micro_rows]
        forward_weights = (
            lax.all_gather(own_shards[0], "shard", axis=0, tiled=True),
            lax.all_gather(own_shards[1], "shard", axis=0, tiled=True),
            lax.all_gather(own_shards[2], "shard", axis=0, tiled=True),
            lax.all_gather(own_shards[3], "shard", axis=0, tiled=True),
            lax.all_gather(own_shards[4], "shard", axis=0, tiled=True),
            lax.all_gather(own_shards[5], "shard", axis=0, tiled=True),
            lax.all_gather(own_shards[6], "shard", axis=0, tiled=True),
            lax.all_gather(own_shards[7], "shard", axis=0, tiled=True),
            lax.all_gather(own_shards[8], "shard", axis=0, tiled=True),
            lax.all_gather(own_shards[9], "shard", axis=0, tiled=True),
        )
        partial_value, saved = forward_pass(
            x_block, forward_weights, qkv_bias, fc1_bias, cos_tab, sin_tab
        )
        branch_total = lax.psum(partial_value.astype(jnp.bfloat16), "tensor").astype(jnp.float32)
        shifts = forward_weights[8].astype(jnp.float32) + forward_weights[9].astype(jnp.float32)
        outputs.append((saved[0] + branch_total + shifts).astype(jnp.bfloat16))
        backward_weights = (
            lax.all_gather(own_shards[0], "shard", axis=0, tiled=True),
            lax.all_gather(own_shards[1], "shard", axis=0, tiled=True),
            lax.all_gather(own_shards[2], "shard", axis=0, tiled=True),
            lax.all_gather(own_shards[3], "shard", axis=0, tiled=True),
            lax.all_gather(own_shards[4], "shard", axis=0, tiled=True),
            lax.all_gather(own_shards[5], "shard", axis=0, tiled=True),
            lax.all_gather(own_shards[6], "shard", axis=0, tiled=True),
            lax.all_gather(own_shards[7], "shard", axis=0, tiled=True),
            lax.all_gather(own_shards[8], "shard", axis=0, tiled=True),
            lax.all_gather(own_shards[9], "shard", axis=0, tiled=True),
        )
        d_input, norm_terms, matrix_grads, shift_grad, qkv_shift_grad, fc1_shift_grad = (
            backward_pass(grad_block, saved, backward_weights, cos_tab, sin_tab)
        )
        summed_input, summed_norms = (
            lax.psum(d_input.astype(jnp.bfloat16), "tensor").astype(jnp.float32),
            lax.psum(norm_terms.astype(jnp.bfloat16), "tensor").astype(jnp.float32),
        )
        grad_outputs.append(grad_block.astype(jnp.float32) + summed_input)
        grad_terms = matrix_grads + (
            summed_norms[0],
            summed_norms[1],
            summed_norms[2],
            summed_norms[3],
            shift_grad,
        )
        grad_accum = grad_terms if micro_index == 0 else add_pairs(grad_accum, grad_terms)
        qkv_shift_acc = qkv_shift_acc + qkv_shift_grad
        fc1_shift_acc = fc1_shift_acc + fc1_shift_grad
    shares = jax.tree.map(
        lambda part: part.astype(jnp.float32),
        lax.psum_scatter(as_sent(grad_accum), "shard", scatter_dimension=0, tiled=True),
    )
    qkv_shift_sum, fc1_shift_sum = lax.psum((qkv_shift_acc, fc1_shift_acc), "shard")
    return (
        jnp.concatenate(outputs, axis=0),
        jnp.concatenate(grad_outputs, axis=0),
        shares[4],
        shares[5],
        shares[0],
        qkv_shift_sum,
        shares[1],
        shares[8],
        shares[6],
        shares[7],
        shares[2],
        fc1_shift_sum,
        shares[3],
        shares[8],
    )


def solution(mesh):
    return jax.shard_map(
        per_device,
        mesh=mesh,
        in_specs=(
            P("shard", None),
            P("shard"),
            P("shard"),
            P("shard", "tensor", None, None),
            P("tensor", None, None),
            P("shard", "tensor", None),
            P("shard"),
            P("shard"),
            P("shard"),
            P("shard", "tensor"),
            P("tensor"),
            P("shard", "tensor"),
            P("shard"),
            P("shard", None),
        ),
        out_specs=(
            P("shard", None),
            P("shard", None),
            P("shard"),
            P("shard"),
            P("shard", "tensor", None, None),
            P("tensor", None, None),
            P("shard", "tensor", None),
            P("shard"),
            P("shard"),
            P("shard"),
            P("shard", "tensor"),
            P("tensor"),
            P("shard", "tensor"),
            P("shard"),
        ),
        check_vma=False,
    )
```

profile of v0, /device:TPU:0, one launch (start us, length us, event | category | flops | bytes accessed | tf_op | source)
XLA Modules:
  0.0 1115.3 jit_solution(9230165923432377804)
XLA Ops:
  9.0 2.1 copy.110
  12.7 10.4 all-gather.3
  23.7 8.9 all-gather.2
  33.2 8.1 all-gather.1
  41.3 8.9 all-gather
  50.8 4.5 convert_reduce_fusion.1
  57.0 2.8 fusion.49
  60.4 6.3 fusion.137
  66.7 5.1 fusion.134
  71.8 17.2 %all-gather.11.cloned.1.call-done = bf16[2048,2,3,256]{3,0,2,1:T(8,128)(2,1)} async-done(((bf16[256,2,3,256]{3,0,2,1:T(8,128)(2,1)}), bf16[2048,2,3,256]{3,0,2,1:T(8,128)(2,1)}) %all-gather.11.cloned.1.call-update) | async-done | bytes 6291472 | tf_op jit(solution)/shard_map/all_gather | solution.py:297
  89.0 11.2 %broadcast_add_fusion = f32[1024,2,3,256]{3,0,2,1:T(8,128)S(1)} fusion(f32[2,3,256]{2,1,0:T(4,128)S(1)} %copy.111, bf16[2048,2,3,256]{3,0,2,1:T(8,128)(2,1)} %all-gather.11.cloned.1.call-done, f32[1024]{0:T(1024)S(1)} %add_rsqrt_fusion, f32[1024]{0:T(1024)S(1)} %get-tuple-element.149, f32[2048]{0:T(1024)S(1)} %bitcast.255, f32[2048]{0:T(1024)S(1)} %bitcast.239, ...), kind=kOutput, calls=%fused_computation.115 | convolution fusion | flops 6456606720 | bytes 16807936 | tf_op jit(solution)/shard_map/md,dhkc->mhkc/dot_general | solution.py:129
  100.7 2.7 copy-done.5
  110.3 6.8 broadcast_add_fusion.1
  119.3 1.9 fusion.213
  125.4 1.8 fusion.167
  127.2 6.5 fusion.128
  133.7 3.5 slice.194
  137.2 5.5 fusion.131
  142.7 2.3 slice.197
  145.7 3.4 multiply_add_fusion.3
  154.5 1.9 fusion.214
  158.1 1.8 fusion.164
  159.9 5.9 fusion.125
  165.8 3.2 convolution_bitcast_fusion
  168.9 4.8 fusion.75
  173.8 4.0 fusion.85
  177.8 14.8 %fusion.146 = f32[2048,2,3,256]{3,0,2,1:T(8,128)} fusion(f32[2048]{0:T(1024)S(1)} %bitcast.257, f32[2048]{0:T(1024)S(1)} %bitcast.241, f32[1024]{0:T(1024)S(1)} %add_rsqrt_fusion.1, f32[1024]{0:T(1024)S(1)} %get-tuple-element.150, f32[1024,2,1,256]{3,0,2,1:T(8,128)} %bitcast.198, f32[1024,2,1,256]{3,0,2,1:T(8,128)} %bitcast.201, ...), kind=kOutput, calls=%fused_computation.178 | convolution fusion | flops 6464471040 | bytes 23093248 | tf_op jit(solution)/shard_map/md,mhkc->dhkc/dot_general | solution.py:239
  192.6 5.7 fusion.122
  198.3 2.0 copy.147
  205.5 15.2 %add_convert_fusion.2 = bf16[2048,2,3,256]{3,0,2,1:T(8,128)(2,1)} fusion(f32[2048,2,3,256]{3,0,2,1:T(8,128)} %fusion.146, f32[1024]{0:T(1024)S(1)} %add_rsqrt_fusion, f32[1024]{0:T(1024)S(1)} %get-tuple-element.149, f32[2048]{0:T(1024)S(1)} %bitcast.258, f32[2048]{0:T(1024)S(1)} %bitcast.242, f32[1024,2,1,256]{3,0,2,1:T(8,128)S(1)} %bitcast.207, ...), kind=kOutput, calls=%fused_computation.5 | convolution fusion | flops 6470762496 | bytes 29384704 | tf_op jit(solution)/shard_map/md,mhkc->dhkc/dot_general | solution.py:239
  221.5 12.8 %fusion.209 = f32[1024,2048]{1,0:T(8,128)S(1)} fusion(bf16[2048,2048]{1,0:T(8,128)(2,1)} %all-gather.15.cloned.1.call-done, f32[1024]{0:T(1024)S(1)} %add_rsqrt_fusion, f32[1024]{0:T(1024)S(1)} %get-tuple-element.149, f32[2048]{0:T(1024)S(1)} %bitcast.251, f32[2048]{0:T(1024)S(1)} %bitcast.232, bf16[2048,2048]{1,0:T(8,128)(2,1)} %param.14), kind=kOutput, calls=%fused_computation.270 | convolution fusion | flops 8602517504 | bytes 20996096 | tf_op jit(solution)/shard_map/dot_general | solution.py:142
  234.2 3.2 copy-done.59
  237.5 15.7 %multiply_convert_fusion.1 = (bf16[1024,2048]{1,0:T(8,128)(2,1)}, bf16[1024,2048]{1,0:T(8,128)(2,1)}, f32[1024,2048]{1,0:T(8,128)}) fusion(f32[2048]{0:T(1024)S(1)} %copy-done.43, f32[1024,2048]{1,0:T(8,128)S(1)} %fusion.209, bf16[2048,2048]{1,0:T(8,128)(2,1)S(1)} %copy-done.49, f32[2048]{0:T(1024)S(1)} %bitcast.252, f32[2048]{0:T(1024)S(1)} %bitcast.233, ...), kind=kOutput, calls=%fused_computation.92 | convolution fusion | flops 8627683328 | bytes 37781504 | tf_op jit(solution)/shard_map/dot_general | solution.py:142
  253.1 18.4 %fusion.215 = (f32[2048]{0:T(1024)}, bf16[1024,2048]{1,0:T(8,128)(2,1)S(1)}) fusion(f32[1024,2048]{1,0:T(8,128)} %get-tuple-element.139, f32[2048]{0:T(1024)S(1)} %copy-done.43, bf16[2048,2048]{1,0:T(8,128)(2,1)} %all-gather.17.cloned.1.call-done, bf16[2048,2048]{1,0:T(8,128)(2,1)} %param.27), kind=kOutput, calls=%fused_computation.275 | convolution fusion | flops 8615098368 | bytes 25182208 | tf_op jit(solution)/shard_map/dot_general | solution.py:207
  271.5 16.8 %fusion.92 = f32[2048,2048]{1,0:T(8,128)} fusion(bf16[1024,2048]{1,0:T(8,128)(2,1)S(1)} %get-tuple-element.146, f32[2048]{0:T(1024)S(1)} %bitcast.253, f32[2048]{0:T(1024)S(1)} %bitcast.234, f32[1024]{0:T(1024)S(1)} %add_rsqrt_fusion.1, f32[1024]{0:T(1024)S(1)} %get-tuple-element.150, bf16[2048,2048]{1,0:T(8,128)(2,1)} %param.14), kind=kOutput, calls=%fused_computation.138 | convolution fusion | flops 8602517504 | bytes 25190400 | tf_op jit(solution)/shard_map/md,mf->df/dot_general | solution.py:210
  288.3 16.6 %fusion.216 = (f32[2048]{0:T(1024)}, bf16[1024,2048]{1,0:T(8,128)(2,1)}) fusion(f32[1024,2048]{1,0:T(8,128)} %copy-done.59, f32[2048]{0:T(1024)S(1)} %copy-done.43, bf16[2048,2048]{1,0:T(8,128)(2,1)S(1)} %copy-done.48, bf16[2048,2048]{1,0:T(8,128)(2,1)} %param.27), kind=kOutput, calls=%fused_computation.276 | convolution fusion | flops 8615098368 | bytes 25182208 | tf_op jit(solution)/shard_map/dot_general | solution.py:207
  305.0 16.8 %add_convert_fusion.1 = bf16[2048,2048]{1,0:T(8,128)(2,1)} fusion(f32[2048,2048]{1,0:T(8,128)} %fusion.92, bf16[1024,2048]{1,0:T(8,128)(2,1)} %get-tuple-element.148, f32[1024]{0:T(1024)S(1)} %add_rsqrt_fusion, f32[1024]{0:T(1024)S(1)} %get-tuple-element.149, f32[2048]{0:T(1024)S(1)} %bitcast.254, f32[2048]{0:T(1024)S(1)} %bitcast.235, ...), kind=kOutput, calls=%fused_computation.4 | convolution fusion | flops 8610906112 | bytes 33579008 | tf_op jit(solution)/shard_map/md,mf->df/dot_general | solution.py:210
  321.9 13.6 %fusion.199 = f32[1024,2048,1,1]{1,0,3,2:T(8,128)} fusion(bf16[2048,2,3,256]{3,0,2,1:T(8,128)(2,1)} %all-gather.11.cloned.1.call-done, f32[1024,2,1,256]{3,0,2,1:T(8,128)} %bitcast.208, f32[1024,2,1,256]{3,0,2,1:T(8,128)} %bitcast.211, f32[1024,2,1,256]{3,0,2,1:T(8,128)} %bitcast.214), kind=kOutput, calls=%fused_computation.264 | convolution fusion | flops 6445596672 | bytes 20971520 | tf_op jit(solution)/shard_map/mhkc,dhkc->md/dot_general | solution.py:242
  335.5 11.4 %fusion.196 = f32[1024,2048,1,1]{1,0,3,2:T(8,128)} fusion(bf16[2048,2,3,256]{3,0,2,1:T(8,128)(2,1)} %all-gather.11.cloned.1.call-done, f32[1024,2,1,256]{3,0,2,1:T(8,128)S(1)} %bitcast.199, f32[1024,2,1,256]{3,0,2,1:T(8,128)S(1)} %bitcast.203, f32[1024,2,1,256]{3,0,2,1:T(8,128)S(1)} %bitcast.206), kind=kOutput, calls=%fused_computation.263 | convolution fusion | flops 6445596672 | bytes 20971520 | tf_op jit(solution)/shard_map/mhkc,dhkc->md/dot_general | solution.py:242
  347.0 11.7 %fusion.118 = f32[2048,2048]{1,0:T(8,128)} fusion(bf16[1024,2048]{1,0:T(8,128)(2,1)S(1)} %copy-done.60, bf16[2048,2048]{1,0:T(8,128)(2,1)S(1)} %bitcast.177), kind=kOutput, calls=%fused_computation.160 | convolution fusion | flops 8589934592 | bytes 25165824 | tf_op jit(solution)/shard_map/md,mf->df/dot_general | solution.py:204
  358.6 16.5 %fusion.64 = bf16[2048,2048]{0,1:T(8,128)(2,1)} fusion(f32[2048,2048]{1,0:T(8,128)} %fusion.118, bf16[1024,2048]{1,0:T(8,128)(2,1)} %get-tuple-element.136, bf16[2048,2048]{1,0:T(8,128)(2,1)S(1)} %bitcast.177), kind=kOutput, calls=%fused_computation.80 | convolution fusion | flops 8598323200 | bytes 33554432 | tf_op jit(solution)/shard_map/md,mf->df/dot_general | solution.py:204
  375.2 15.0 %fusion.94 = f32[1024,2048]{1,0:T(8,128)} fusion(bf16[2048,2048]{1,0:T(8,128)(2,1)} %all-gather.15.cloned.1.call-done, bf16[1024,2048]{1,0:T(8,128)(2,1)} %copy-done.62), kind=kOutput, calls=%fused_computation.140 | convolution fusion | flops 8589934592 | bytes 20971520 | tf_op jit(solution)/shard_map/mf,df->md/dot_general | solution.py:211
  390.2 30.2 %fusion.34 = (bf16[2048]{0:T(1024)(128)(2,1)S(1)}, f32[1024]{0:T(1024)S(1)}, f32[1024]{0:T(1024)S(1)}, bf16[2048]{0:T(1024)(128)(2,1)S(1)}, f32[1024]{0:T(1024)S...) fusion(f32[1024]{0:T(1024)S(1)} %add_rsqrt_fusion, ...), kind=kOutput, calls=%fused_computation.50 | convolution fusion | flops 8661213184 | bytes 54624256 | tf_op jit(solution)/shard_map/mf,df->md/dot_general | solution.py:211
  420.5 12.5 %fusion.217 = f32[1024,2048]{1,0:T(8,128)S(1)} fusion(bf16[1024,2048]{1,0:T(8,128)(2,1)S(1)} %copy-done.61, bf16[2048,2048]{1,0:T(8,128)(2,1)} %all-gather.17.cloned.1.call-done), kind=kOutput, calls=%fused_computation.277 | convolution fusion | flops 8589934592 | bytes 20971520 | tf_op jit(solution)/shard_map/mf,df->md/dot_general | solution.py:149
  433.1 4.4 fusion.66
  437.4 14.8 %fusion.218 = f32[1024,2048]{1,0:T(8,128)} fusion(bf16[1024,2048]{1,0:T(8,128)(2,1)} %get-tuple-element.136, bf16[2048,2048]{1,0:T(8,128)(2,1)} %all-gather.17.cloned.1.call-done), kind=kOutput, calls=%fused_computation.278 | convolution fusion | flops 8589934592 | bytes 20971520 | tf_op jit(solution)/shard_map/mf,df->md/dot_general | solution.py:149
  452.2 8.5 fusion.65
  460.8 8.4 fusion.44
  469.1 8.1 fusion.30
  479.2 7.9 all-gather.5
  487.1 9.2 all-gather.4
  496.3 2.6 fusion.71
  499.4 1.9 copy.157
  501.3 26.1 %all-reduce.5 = (f32[2,3,256]{2,1,0:T(4,128)S(1)}, f32[2048]{0:T(1024)}) all-reduce(f32[2,3,256]{2,1,0:T(4,128)S(1)} %add.284, f32[2048]{0:T(1024)S(1)} %add.290), channel_id=1, replica_groups=mesh['shard'=8,'tensor'=4] {'shard'}, use_global_device_ids=true, to_apply=%region_37.38 | all-reduce | flops 3584 | bytes 28672 | tf_op jit(solution)/shard_map/psum | solution.py:348
  528.2 21.2 %all-reduce.7 = (bf16[4,2048]{1,0:T(4,128)(2,1)S(1)}, bf16[4,2048]{1,0:T(4,128)(2,1)S(1)}) all-reduce(bf16[4,2048]{1,0:T(4,128)(2,1)S(1)} %pad_maximum_fusion.13, bf16[4,2048]{1,0:T(4,128)(2,1)S(1)} %pad_maximum_fusion.12), channel_id=1, replica_groups=mesh['shard'=8,'tensor'=4] {'tensor'}, use_global_device_ids=true, to_apply=%region_31.32 | all-reduce | flops 16384 | bytes 65536 | tf_op jit(solution)/shard_map/psum | solution.py:331
  549.6 3.1 copy.155
  552.7 2.8 convert_element_type.300
  555.5 2.6 copy.158
  558.1 481.4 %all-reduce.11.cloned.1.call-done = (bf16[1024,2048]{1,0:T(8,128)(2,1)}, bf16[1024,2048]{1,0:T(8,128)(2,1)}, bf16[1024,2048]{1,0:T(8,128)(2,1)}, bf16[1024,2048]{1,0:T(8,128)(2,1)}) async-done(((bf16[1024,2048]{1,0:T(8,128)(2,1)}, bf16[1024,2048]{1,0:T(8,128)(2,1)}, bf16[1024,2048]{1,0:T(8,128)(2,1)}, bf16[1024,2048]{1,0:T(8,128)(2,1)}), (bf16[1024,2048]{1,0:T(8,128)(2,1)}, bf16[1024,2048]{1,0:T(8,128)(2,1)}, ...) | async-done | bytes 16777232 | tf_op jit(solution)/shard_map/psum | solution.py:311
  1039.5 11.3 %convert_reduce_fusion.2 = (f32[2048]{0:T(1024)S(1)}, f32[2048]{0:T(1024)S(1)}, f32[1024,2048]{1,0:T(8,128)}, f32[1024,2048]{1,0:T(8,128)}) fusion(bf16[2048,2048]{1,0:T(8,128)(2,1)} %param.27, bf16[1024,2048]{1,0:T(8,128)(2,1)} %get-tuple-element.99, bf16[1024,2048]{1,0:T(8,128)(2,1)} %get-tuple-element.100), kind=kLoop, calls=%fused_computation.14 | loop fusion | flops 16773120 | bytes 33570816 | tf_op jit(solution)/shard_map/reduce_sum | solution.py:202
  1050.8 23.8 %all-reduce.6 = (bf16[2048]{0:T(1024)(128)(2,1)S(1)}, bf16[2048]{0:T(1024)(128)(2,1)S(1)}, bf16[2048]{0:T(1024)(128)(2,1)S(1)}, bf16[2048]{0:T(1024)(128)(2,1)S(1)}, bf16[2048]{0:T(1024)(128)(2,1)S(1)}) all-reduce(bf16[2048]{0:T(1024)(128)(2,1)S(1)} %get-tuple-element.87, ...), channel_id=2, replica_groups=mesh['shard'=8,'tensor'=4] {'shard'}, use_global_device_ids=true, to_apply=%region_32.33.clone | all-reduce | flops 10240 | bytes 40960
  1077.2 10.2 fusion.51
  1087.4 8.5 pad_maximum_fusion.1
  1096.0 11.8 %pad_maximum_fusion = f32[2048,2048]{1,0:T(8,128)} fusion(f32[1024,2048]{1,0:T(8,128)} %get-tuple-element.103, f32[1024,2048]{1,0:T(8,128)} %get-tuple-element.104), kind=kLoop, calls=%fused_computation.2 | loop fusion | flops 4194304 | bytes 33554432 | tf_op jit(solution)/shard_map/concatenate | solution.py:351
  (279 shorter events, 40.2 us)
Async XLA Ops:
  7.2 5.4 copy-start.52
  7.2 5.4 copy-start.53
  7.2 5.4 copy-start.54
  7.2 5.4 copy-start.55
  7.2 43.0 %copy-start.45 = (bf16[2048]{0:T(1024)(128)(2,1)S(1)}, bf16[2048]{0:T(1024)(128)(2,1)}, u32[]{:S(2)}) copy-start(bf16[2048]{0:T(1024)(128)(2,1)} %param.24) | copy-start | bytes 12292
  7.2 43.6 %copy-start.47 = (bf16[2,3,256]{2,0,1:T(2,128)(2,1)S(1)}, bf16[2,3,256]{2,0,1:T(2,128)(2,1)}, u32[]{:S(2)}) copy-start(bf16[2,3,256]{2,0,1:T(2,128)(2,1)} %param.18) | copy-start | bytes 9220
  7.2 53.1 %all-gather.13.cloned.1.call-start = ((), (), s32[]{:S(2)}) async-start(), calls=%async_computation.5 | async-start | bytes 2359296 | tf_op jit(solution)/shard_map/all_gather | solution.py:298
  9.0 80.0 %all-gather.11.cloned.1.call-start = ((), (), s32[]{:S(2)}) async-start(), calls=%async_computation.4 | async-start | bytes 7077888 | tf_op jit(solution)/shard_map/all_gather | solution.py:297
  11.2 209.7 %all-gather.15.cloned.1.call-start = ((), (), s32[]{:S(2)}) async-start(), calls=%async_computation.6 | async-start | bytes 9437184 | tf_op jit(solution)/shard_map/all_gather | solution.py:299
  11.9 241.2 %all-gather.17.cloned.1.call-start = ((), (), s32[]{:S(2)}) async-start(), calls=%async_computation.7 | async-start | bytes 9437184 | tf_op jit(solution)/shard_map/all_gather | solution.py:300
  12.5 486.9 %reduce-scatter.7.cloned.1.call-start = ((), (), s32[]{:S(2)}) async-start(), calls=%async_computation.9 | async-start | bytes 2359296 | tf_op jit(solution)/shard_map/reduce_scatter | solution.py:346
  50.2 155.3 %copy-start.39 = (f32[8,1,256]{2,1,0:T(1,128)}, f32[8,1,256]{2,1,0:T(1,128)S(1)}, u32[]{:S(2)}) copy-start(f32[8,1,256]{2,1,0:T(1,128)S(1)} %convert_element_type.304) | copy-start | bytes 24580
  50.8 6.2 copy-start
  60.4 6.3 copy-start.50
  100.2 8.9 slice-start
  100.2 8.9 slice-start.16
  103.4 5.9 slice-start.1
  103.4 6.8 slice-start.17
  127.2 10.0 copy-start.28
  149.2 5.3 copy-start.30
  149.2 5.3 copy-start.31
  149.2 5.3 copy-start.32
  149.2 5.3 copy-start.33
  153.0 3.8 slice-start.10
  158.0 11.0 copy-start.19
  165.8 8.0 slice-start.6
  168.9 4.8 slice-start.7
  168.9 4.8 copy-start.22
  177.8 371.8 %reduce-scatter.5.cloned.1.call-start = ((), (), s32[]{:S(2)}) async-start(), calls=%async_computation.8 | async-start | bytes 7077888 | tf_op jit(solution)/shard_map/reduce_scatter | solution.py:346
  177.8 14.8 %copy-start.25 = (bf16[4,256,2,192]{3,1,2,0:T(8,128)(2,1)S(1)}, bf16[4,256,2,192]{3,1,2,0:T(8,128)(2,1)}, u32[]{:S(2)}) copy-start(bf16[4,256,2,192]{3,1,2,0:T(8,128)(2,1)} %slice.350) | copy-start | bytes 2359300
  200.5 5.0 copy-start.11
  205.5 15.3 %copy-start.15 = (f32[4,256,2,256]{3,1,0,2:T(8,128)}, f32[4,256,2,256]{3,1,0,2:T(8,128)S(1)}, u32[]{:S(2)}) copy-start(f32[4,256,2,256]{3,1,0,2:T(8,128)S(1)} %copy.141) | copy-start | bytes 6291460
  220.8 331.9 %reduce-scatter.9.cloned.1.call-start = ((), (), s32[]{:S(2)}) async-start(), calls=%async_computation.10 | async-start | bytes 9437184 | tf_op jit(solution)/shard_map/reduce_scatter | solution.py:346
  221.5 16.0 %copy-start.43 = (f32[2048]{0:T(1024)S(1)}, f32[2048]{0:T(1024)}, u32[]{:S(2)}) copy-start(f32[2048]{0:T(1024)} %convert_element_type.246) | copy-start | bytes 24580
  221.5 16.0 %copy-start.49 = (bf16[2048,2048]{1,0:T(8,128)(2,1)S(1)}, bf16[2048,2048]{1,0:T(8,128)(2,1)}, u32[]{:S(2)}) copy-start(bf16[2048,2048]{1,0:T(8,128)(2,1)} %all-gather.15.cloned.1.call-done) | copy-start | bytes 25165828
  234.2 3.2 copy-start.59
  271.5 16.8 %copy-start.62 = (bf16[1024,2048]{1,0:T(8,128)(2,1)}, bf16[1024,2048]{1,0:T(8,128)(2,1)S(1)}, u32[]{:S(2)}) copy-start(bf16[1024,2048]{1,0:T(8,128)(2,1)S(1)} %get-tuple-element.146) | copy-start | bytes 12582916
  271.5 16.8 %copy-start.48 = (bf16[2048,2048]{1,0:T(8,128)(2,1)S(1)}, bf16[2048,2048]{1,0:T(8,128)(2,1)}, u32[]{:S(2)}) copy-start(bf16[2048,2048]{1,0:T(8,128)(2,1)} %all-gather.17.cloned.1.call-done) | copy-start | bytes 25165828
  271.5 33.4 %slice-start.2 = ((s8[8388608]{0:T(1024)(128)(4,1)}), s8[4194304]{0:T(1024)(128)(4,1)S(1)}, s32[]{:S(2)}) async-start(s8[8388608]{0:T(1024)(128)(4,1)} %bitcast.170), calls=%async_computation.15 | async-start | bytes 8388608
  288.3 16.6 %slice-start.3 = ((s8[8388608]{0:T(1024)(128)(4,1)}), s8[4194304]{0:T(1024)(128)(4,1)S(1)}, s32[]{:S(2)}) async-start(s8[8388608]{0:T(1024)(128)(4,1)} %bitcast.170), calls=%async_computation.16 | async-start | bytes 8388608
  321.8 13.7 %copy-start.7 = (f32[4,256,2,256]{3,1,0,2:T(8,128)S(1)}, f32[4,256,2,256]{3,1,0,2:T(8,128)}, u32[]{:S(2)}) copy-start(f32[4,256,2,256]{3,1,0,2:T(8,128)} %copy.133) | copy-start | bytes 6291460
  321.8 233.7 %reduce-scatter.11.cloned.1.call-start = ((), (), s32[]{:S(2)}) async-start(), calls=%async_computation.11 | async-start | bytes 9437184 | tf_op jit(solution)/shard_map/reduce_scatter | solution.py:346
  321.8 13.7 %copy-start.9 = (f32[4,256,2,256]{3,1,0,2:T(8,128)S(1)}, f32[4,256,2,256]{3,1,0,2:T(8,128)}, u32[]{:S(2)}) copy-start(f32[4,256,2,256]{3,1,0,2:T(8,128)} %copy.131) | copy-start | bytes 6291460
  321.8 13.7 %copy-start.10 = (f32[4,256,2,256]{3,1,0,2:T(8,128)S(1)}, f32[4,256,2,256]{3,1,0,2:T(8,128)}, u32[]{:S(2)}) copy-start(f32[4,256,2,256]{3,1,0,2:T(8,128)} %copy.127) | copy-start | bytes 6291460
  321.8 25.1 %slice-start.8 = ((s8[8388608]{0:T(1024)(128)(4,1)}), s8[4194304]{0:T(1024)(128)(4,1)S(1)}, s32[]{:S(2)}) async-start(s8[8388608]{0:T(1024)(128)(4,1)} %bitcast.176), calls=%async_computation.21 | async-start | bytes 8388608
  335.5 11.5 %slice-start.9 = ((s8[8388608]{0:T(1024)(128)(4,1)}), s8[4194304]{0:T(1024)(128)(4,1)S(1)}, s32[]{:S(2)}) async-start(s8[8388608]{0:T(1024)(128)(4,1)} %bitcast.176), calls=%async_computation.22 | async-start | bytes 8388608
  335.5 11.4 %copy-start.60 = (bf16[1024,2048]{1,0:T(8,128)(2,1)S(1)}, bf16[1024,2048]{1,0:T(8,128)(2,1)}, u32[]{:S(2)}) copy-start(bf16[1024,2048]{1,0:T(8,128)(2,1)} %get-tuple-element.135) | copy-start | bytes 12582916
  375.1 15.0 %copy-start.40 = (f32[8,1,256]{2,1,0:T(1,128)S(1)}, f32[8,1,256]{2,1,0:T(1,128)}, u32[]{:S(2)}) copy-start(f32[8,1,256]{2,1,0:T(1,128)} %copy-done.39) | copy-start | bytes 24580
  375.1 664.3 %all-reduce.11.cloned.1.call-start = ((), (), s32[]{:S(2)}) async-start(), calls=%async_computation.12 | async-start | bytes 33554432 | tf_op jit(solution)/shard_map/psum | solution.py:311
  390.2 30.3 %copy-start.61 = (bf16[1024,2048]{1,0:T(8,128)(2,1)S(1)}, bf16[1024,2048]{1,0:T(8,128)(2,1)}, u32[]{:S(2)}) copy-start(bf16[1024,2048]{1,0:T(8,128)(2,1)} %get-tuple-element.135) | copy-start | bytes 12582916
  420.5 12.6 %copy-start.23 = (bf16[4,256,2,256]{3,1,0,2:T(8,128)(2,1)S(1)}, bf16[4,256,2,256]{3,1,0,2:T(8,128)(2,1)}, u32[]{:S(2)}) copy-start(bf16[4,256,2,256]{3,1,0,2:T(8,128)(2,1)} %copy.116) | copy-start | bytes 3145732
  420.5 12.6 %copy-start.51 = (bf16[2048,2,256]{2,0,1:T(8,128)(2,1)S(1)}, bf16[2048,2,256]{2,0,1:T(8,128)(2,1)}, u32[]{:S(2)}) copy-start(bf16[2048,2,256]{2,0,1:T(8,128)(2,1)} %all-gather.13.cloned.1.call-done) | copy-start | bytes 6291460
  433.0 27.7 %slice-start.4 = ((s8[8388608]{0:T(1024)(128)(4,1)}), s8[4194304]{0:T(1024)(128)(4,1)S(1)}, s32[]{:S(2)}) async-start(s8[8388608]{0:T(1024)(128)(4,1)} %bitcast.172), calls=%async_computation.17 | async-start | bytes 8388608
  433.1 27.7 %slice-start.14 = ((s8[8388608]{0:T(1024)(128)(4,1)}), s8[4194304]{0:T(1024)(128)(4,1)S(1)}, s32[]{:S(2)}) async-start(s8[8388608]{0:T(1024)(128)(4,1)} %bitcast.196), calls=%async_computation.27 | async-start | bytes 8388608
  437.4 14.8 %copy-start.20 = (bf16[4,256,2,256]{3,1,0,2:T(8,128)(2,1)S(1)}, bf16[4,256,2,256]{3,1,0,2:T(8,128)(2,1)}, u32[]{:S(2)}) copy-start(bf16[4,256,2,256]{3,1,0,2:T(8,128)(2,1)} %copy-done.19) | copy-start | bytes 3145732
  437.4 23.3 %slice-start.5 = ((s8[8388608]{0:T(1024)(128)(4,1)}), s8[4194304]{0:T(1024)(128)(4,1)S(1)}, s32[]{:S(2)}) async-start(s8[8388608]{0:T(1024)(128)(4,1)} %bitcast.172), calls=%async_computation.18 | async-start | bytes 8388608
  437.4 23.3 %slice-start.15 = ((s8[8388608]{0:T(1024)(128)(4,1)}), s8[4194304]{0:T(1024)(128)(4,1)S(1)}, s32[]{:S(2)}) async-start(s8[8388608]{0:T(1024)(128)(4,1)} %bitcast.196), calls=%async_computation.28 | async-start | bytes 8388608
  452.2 16.9 %slice-start.12 = ((s8[8388608]{0:T(1024)(128)(4,1)}), s8[4194304]{0:T(1024)(128)(4,1)S(1)}, s32[]{:S(2)}) async-start(s8[8388608]{0:T(1024)(128)(4,1)} %bitcast.194), calls=%async_computation.25 | async-start | bytes 8388608
  460.8 8.4 slice-start.13
  477.3 19.1 %copy-start.8 = (f32[4,256,2,256]{3,1,0,2:T(8,128)S(1)}, f32[4,256,2,256]{3,1,0,2:T(8,128)}, u32[]{:S(2)}) copy-start(f32[4,256,2,256]{3,1,0,2:T(8,128)} %copy.133) | copy-start | bytes 6291460
  479.2 19.8 %copy-start.12 = (f32[4,256,2,256]{3,1,0,2:T(8,128)S(1)}, f32[4,256,2,256]{3,1,0,2:T(8,128)}, u32[]{:S(2)}) copy-start(f32[4,256,2,256]{3,1,0,2:T(8,128)} %copy-done.11) | copy-start | bytes 6291460
  479.2 19.8 %copy-start.14 = (f32[4,256,2,256]{3,1,0,2:T(8,128)S(1)}, f32[4,256,2,256]{3,1,0,2:T(8,128)}, u32[]{:S(2)}) copy-start(f32[4,256,2,256]{3,1,0,2:T(8,128)} %copy-done.13) | copy-start | bytes 6291460
  479.2 19.8 %copy-start.16 = (f32[4,256,2,256]{3,1,0,2:T(8,128)S(1)}, f32[4,256,2,256]{3,1,0,2:T(8,128)}, u32[]{:S(2)}) copy-start(f32[4,256,2,256]{3,1,0,2:T(8,128)} %copy-done.15) | copy-start | bytes 6291460
  1075.3 32.5 %copy-start.46 = (f32[256]{0:T(256)}, f32[256]{0:T(256)S(1)}, u32[]{:S(2)}) copy-start(f32[256]{0:T(256)S(1)} %dynamic-slice_convert_fusion.2) | copy-start | bytes 3076
  (26 other events, 51.1 us)
Sparse Core Ops, SparseCore 0:
  10.5 30.5 all-gather.12
  43.6 45.3 all-gather.10
  90.9 54.2 all-gather.14
  146.9 54.2 all-gather.16
  204.3 41.1 reduce-scatter.6
  248.7 61.5 reduce-scatter.4
  321.9 71.3 reduce-scatter.8
  396.8 71.2 reduce-scatter.10
  477.4 562.0 all-reduce.10
where the time goes:
time: 1120 us
  waiting for transfers between devices  500 us (45%)
  matrix products  340 us (30%)
  blocking collectives  125 us (11%)
  other arithmetic  87.2 us (8%)
  local copies, waits for them, and re-layouts  47.4 us (4%)
  between operations  16.2 us (1%)
    psum x1, waiting for transfers between devices, per_device(): lax.psum(partial_value.astype(jnp.bfloat16), 'tensor').astype(jnp.float32)  481 us
    dot_general x2, matrix products, backward_pass(): jnp.einsum('mf,df->md', d_pre_b, fc1_full, preferred_element_type=jnp.flo...  45.1 us
    dot_general x2, matrix products, backward_pass(): jnp.dot(grad_block, fc2_full, preferred_element_type=jnp.float32)  35 us
    dot_general x2, matrix products, backward_pass(): jnp.einsum('md,mf->df', normed_two, d_pre_b, preferred_element_type=jnp.f...  33.6 us
    dot_general x2, matrix products, backward_pass(): jnp.einsum('md,mhkc->dhkc', normed_one, d_qkv_b, preferred_element_type=j...  30 us
    dot_general x2, matrix products, forward_pass(): jnp.dot(normed_two, fc1_full, preferred_element_type=jnp.float32)  28.4 us
    unnamed x180, local copies, waits for them, and re-layouts  28.2 us
    dot_general x2, matrix products, backward_pass(): jnp.einsum('md,mf->df', grad_block, hidden, preferred_element_type=jnp.fl...  28.2 us
  transfers between devices with their start and end apart: 9, of which 2 were waited for; matrix products, arithmetic and copies ran while one was open for 37% of the time, Pallas kernels for 0%

commit v1 on v0

--- a/solution.py
+++ b/solution.py
@@ -10,6 +10,7 @@
 NORM_EPS = 1e-05
 ROOT_HALF = 0.7071067811865476
 INV_ROOT_TWO_PI = 0.3989422804014327
+bring_plane_now = lambda matrix: jnp.sum(lax.all_gather(matrix, "tensor"), 0)
 
 
 def as_sent(shard):
@@ -308,7 +309,7 @@
         partial_value, saved = forward_pass(
             x_block, forward_weights, qkv_bias, fc1_bias, cos_tab, sin_tab
         )
-        branch_total = lax.psum(partial_value.astype(jnp.bfloat16), "tensor").astype(jnp.float32)
+        branch_total = bring_plane_now(partial_value.astype(jnp.bfloat16)).astype(jnp.float32)
         shifts = forward_weights[8].astype(jnp.float32) + forward_weights[9].astype(jnp.float32)
         outputs.append((saved[0] + branch_total + shifts).astype(jnp.bfloat16))
         backward_weights = (

time: 1120 us -> 1410 us (1.26)
  waiting for transfers between devices: 500 us -> 762 us
  other arithmetic: 87.2 us -> 119 us
    all_gather x0 -> x2, waiting for transfers between devices: none -> 265 us  [lax.all_gather(matrix, 'tensor')]
    psum x1, waiting for transfers between devices: 481 us -> 282 us  [per_device(): lax.psum(d_input.astype(jnp.bfloat16), 'tensor').astype(jnp.float32)]
    reduce_scatter x4, waiting for transfers between devices: 0.05 us -> 168 us  [per_device(): lax.psum_scatter(as_sent(grad_accum), 'shard', scatter_dimension=0, tiled...]
    reduce_sum x0 -> x2, other arithmetic: none -> 25.6 us  [jnp.sum(lax.all_gather(matrix, 'tensor'), 0)]
    all_gather x1, waiting for transfers between devices: 0.01 us -> 20.8 us  [per_device(): lax.all_gather(own_shards[3], 'shard', axis=0, tiled=True)]
    unnamed x180 -> x182, local copies, waits for them, and re-layouts: 28.2 us -> 33 us
  transfers between devices with their start and end apart: 9 -> 11, of which waited for: 2 -> 8; matrix products, arithmetic and copies ran while one was open for 37% -> 31% of each run, Pallas kernels for 0% -> 0%
where the time goes in v1:
time: 1410 us; the launch traced here: 1400 us
  waiting for transfers between devices  762 us (54%)
  matrix products  334 us (24%)
  blocking collectives  120 us (9%)
  other arithmetic  119 us (8%)
  local copies, waits for them, and re-layouts  47.4 us (3%)
  between operations  16 us (1%)
    psum x1, waiting for transfers between devices, per_device(): lax.psum(d_input.astype(jnp.bfloat16), 'tensor').astype(jnp.float32)  282 us
    all_gather x2, waiting for transfers between devices, lax.all_gather(matrix, 'tensor')  265 us
    reduce_scatter x4, waiting for transfers between devices, per_device(): lax.psum_scatter(as_sent(grad_accum), 'shard', scatter_dimension=0, tiled...  168 us
    dot_general x2, matrix products, backward_pass(): jnp.einsum('mf,df->md', d_pre_b, fc1_full, preferred_element_type=jnp.flo...  39.3 us
    dot_general x2, matrix products, backward_pass(): jnp.dot(grad_block, fc2_full, preferred_element_type=jnp.float32)  35.5 us
    unnamed x182, local copies, waits for them, and re-layouts  33 us
    dot_general x2, matrix products, backward_pass(): jnp.einsum('md,mf->df', normed_two, d_pre_b, preferred_element_type=jnp.f...  31.8 us
    dot_general x2, matrix products, backward_pass(): jnp.einsum('md,mf->df', grad_block, hidden, preferred_element_type=jnp.fl...  31.5 us
  transfers between devices with their start and end apart: 11, of which 8 were waited for; matrix products, arithmetic and copies ran while one was open for 31% of the time, Pallas kernels for 0%

profile of v1, /device:TPU:0, one launch (start us, length us, event | category | flops | bytes accessed | tf_op | source)
XLA Modules:
  0.0 1399.3 jit_solution(8799751059579448121)
XLA Ops:
  12.7 10.4 all-gather.5
  23.1 8.9 all-gather.4
  32.1 8.2 all-gather.3
  40.3 8.9 all-gather.2
  49.3 4.9 convert_reduce_fusion.1
  55.9 2.8 fusion.49
  59.2 5.2 fusion.134
  64.5 24.5 %all-gather.15.cloned.1.call-done = bf16[2048,2,3,256]{3,0,2,1:T(8,128)(2,1)} async-done(((bf16[256,2,3,256]{3,0,2,1:T(8,128)(2,1)}), bf16[2048,2,3,256]{3,0,2,1:T(8,128)(2,1)}) %all-gather.15.cloned.1.call-update) | async-done | bytes 6291472 | tf_op jit(solution)/shard_map/all_gather | solution.py:298
  89.0 11.5 broadcast_add_fusion
  100.9 2.8 copy-done.5
  110.5 6.8 broadcast_add_fusion.1
  125.2 6.1 fusion.131
  131.3 5.8 fusion.128
  137.1 7.0 multiply_add_fusion.3
  148.6 12.8 fusion.209
  161.4 3.2 copy-done.72
  164.6 15.8 %multiply_convert_fusion.1 = (bf16[1024,2048]{1,0:T(8,128)(2,1)}, bf16[1024,2048]{1,0:T(8,128)(2,1)}, f32[1024,2048]{1,0:T(8,128)}) fusion(f32[2048]{0:T(1024)S(1)} %convert_element_type.250, f32[1024,2048]{1,0:T(8,128)S(1)} %fusion.209, bf16[2048,2048]{1,0:T(8,128)(2,1)S(1)} %copy-done.61, f32[2048]{0:T(1024)S(1)} %bitcast.232, f32[2048]{0:T(1024)S(1)} %bitcast.213, ...), kind=kOutput, calls=%fused_computation.92 | convolution fusion | flops 8627683328 | bytes 37781504 | tf_op jit(solution)/shard_map/dot_general | solution.py:143
  180.4 20.8 %all-gather.21.cloned.1.call-done = bf16[2048,2048]{1,0:T(8,128)(2,1)} async-done(((bf16[256,2048]{1,0:T(8,128)(2,1)}), bf16[2048,2048]{1,0:T(8,128)(2,1)}) %all-gather.21.cloned.1.call-update) | async-done | bytes 8388624 | tf_op jit(solution)/shard_map/all_gather | solution.py:301
  201.2 12.7 fusion.218
  213.9 4.4 fusion.65
  218.4 3.0 fusion.140
  221.9 11.4 fusion.217
  233.3 4.4 fusion.66
  238.2 5.3 fusion.137
  253.7 3.4 fusion.164
  257.1 5.7 fusion.125
  262.8 3.0 convolution_bitcast_fusion
  265.8 4.7 fusion.75
  270.6 6.3 fusion.85
  277.0 14.8 %fusion.146 = f32[2048,2,3,256]{3,0,2,1:T(8,128)} fusion(f32[2048]{0:T(1024)S(1)} %bitcast.237, f32[2048]{0:T(1024)S(1)} %bitcast.221, f32[1024]{0:T(1024)S(1)} %add_rsqrt_fusion.1, f32[1024]{0:T(1024)S(1)} %broadcast_multiply_fusion.9, f32[1024,2,1,256]{3,0,2,1:T(8,128)} %bitcast.178, f32[1024,2,1,256]{3,0,2,1:T(8,128)} %bitcast.181, ...), kind=kOutput, calls=%fused_computation.178 | convolution fusion | flops 6464471040 | bytes 23093248 | tf_op jit(solution)/shard_map/md,mhkc->dhkc/dot_general | solution.py:240
  291.7 5.7 fusion.122
  304.6 15.3 %add_convert_fusion.2 = bf16[2048,2,3,256]{3,0,2,1:T(8,128)(2,1)} fusion(f32[2048,2,3,256]{3,0,2,1:T(8,128)} %fusion.146, f32[1024]{0:T(1024)S(1)} %add_rsqrt_fusion, f32[1024]{0:T(1024)S(1)} %broadcast_multiply_fusion.8, f32[2048]{0:T(1024)S(1)} %bitcast.238, f32[2048]{0:T(1024)S(1)} %bitcast.222, f32[1024,2,1,256]{3,0,2,1:T(8,128)S(1)} %bitcast.187, ...), kind=kOutput, calls=%fused_computation.5 | convolution fusion | flops 6470762496 | bytes 29384704 | tf_op jit(solution)/shard_map/md,mhkc->dhkc/dot_general | solution.py:240
  319.9 16.8 %fusion.215 = (f32[2048]{0:T(1024)}, bf16[1024,2048]{1,0:T(8,128)(2,1)S(1)}) fusion(f32[1024,2048]{1,0:T(8,128)} %get-tuple-element.138, f32[2048]{0:T(1024)S(1)} %convert_element_type.250, bf16[2048,2048]{1,0:T(8,128)(2,1)} %all-gather.21.cloned.1.call-done, bf16[2048,2048]{1,0:T(8,128)(2,1)} %param.27), kind=kOutput, calls=%fused_computation.275 | convolution fusion | flops 8615098368 | bytes 25182208 | tf_op jit(solution)/shard_map/dot_general | solution.py:208
  338.7 15.1 %fusion.92 = f32[2048,2048]{1,0:T(8,128)} fusion(bf16[1024,2048]{1,0:T(8,128)(2,1)S(1)} %get-tuple-element.145, f32[2048]{0:T(1024)S(1)} %bitcast.233, f32[2048]{0:T(1024)S(1)} %bitcast.214, f32[1024]{0:T(1024)S(1)} %add_rsqrt_fusion.1, f32[1024]{0:T(1024)S(1)} %broadcast_multiply_fusion.9, bf16[2048,2048]{1,0:T(8,128)(2,1)} %param.14), kind=kOutput, calls=%fused_computation.138 | convolution fusion | flops 8602517504 | bytes 25190400 | tf_op jit(solution)/shard_map/md,mf->df/dot_general | solution.py:211
  353.8 18.7 %fusion.216 = (f32[2048]{0:T(1024)}, bf16[1024,2048]{1,0:T(8,128)(2,1)}) fusion(f32[1024,2048]{1,0:T(8,128)} %copy-done.72, f32[2048]{0:T(1024)S(1)} %convert_element_type.250, bf16[2048,2048]{1,0:T(8,128)(2,1)} %all-gather.21.cloned.1.call-done, bf16[2048,2048]{1,0:T(8,128)(2,1)} %param.27), kind=kOutput, calls=%fused_computation.276 | convolution fusion | flops 8615098368 | bytes 25182208 | tf_op jit(solution)/shard_map/dot_general | solution.py:208
  372.5 16.7 %add_convert_fusion.1 = bf16[2048,2048]{1,0:T(8,128)(2,1)} fusion(f32[2048,2048]{1,0:T(8,128)} %fusion.92, bf16[1024,2048]{1,0:T(8,128)(2,1)} %get-tuple-element.147, f32[1024]{0:T(1024)S(1)} %add_rsqrt_fusion, f32[1024]{0:T(1024)S(1)} %broadcast_multiply_fusion.8, f32[2048]{0:T(1024)S(1)} %bitcast.234, f32[2048]{0:T(1024)S(1)} %bitcast.215, ...), kind=kOutput, calls=%fused_computation.4 | convolution fusion | flops 8610906112 | bytes 33579008 | tf_op jit(solution)/shard_map/md,mf->df/dot_general | solution.py:211
  389.9 9.0 all-gather.7
  398.9 8.1 all-gather.6
  407.0 15.7 %fusion.118 = f32[2048,2048]{1,0:T(8,128)} fusion(bf16[1024,2048]{1,0:T(8,128)(2,1)} %get-tuple-element.134, bf16[2048,2048]{1,0:T(8,128)(2,1)} %param.27), kind=kOutput, calls=%fused_computation.160 | convolution fusion | flops 8589934592 | bytes 25165824 | tf_op jit(solution)/shard_map/md,mf->df/dot_general | solution.py:205
  422.7 15.8 %fusion.64 = bf16[2048,2048]{0,1:T(8,128)(2,1)} fusion(f32[2048,2048]{1,0:T(8,128)} %fusion.118, bf16[1024,2048]{1,0:T(8,128)(2,1)S(1)} %copy-done.71, bf16[2048,2048]{1,0:T(8,128)(2,1)} %param.27), kind=kOutput, calls=%fused_computation.80 | convolution fusion | flops 8598323200 | bytes 33554432 | tf_op jit(solution)/shard_map/md,mf->df/dot_general | solution.py:205
  438.6 13.0 fusion.199
  451.7 11.0 fusion.196
  462.7 11.1 fusion.94
  473.8 28.2 %fusion.34 = (bf16[2048]{0:T(1024)(128)(2,1)S(1)}, f32[1024]{0:T(1024)S(1)}, f32[1024]{0:T(1024)S(1)}, bf16[2048]{0:T(1024)(128)(2,1)S(1)}, f32[1024]{0:T(1024)S...) fusion(f32[1024]{0:T(1024)S(1)} %add_rsqrt_fusion, ...), kind=kOutput, calls=%fused_computation.50 | convolution fusion | flops 8661213184 | bytes 54624256 | tf_op jit(solution)/shard_map/mf,df->md/dot_general | solution.py:212
  502.1 11.2 fusion.30
  513.3 13.4 reduce_sum.301
  526.7 265.0 %all-gather.23.cloned.1.call-done = bf16[4096,2048]{1,0:T(8,128)(2,1)} async-done(((bf16[1024,2048]{1,0:T(8,128)(2,1)}), bf16[4096,2048]{1,0:T(8,128)(2,1)}) %all-gather.23.cloned.1.call-update) | async-done | bytes 16777232 | tf_op jit(solution)/shard_map/all_gather | solution.py:13
  791.7 12.2 reduce_sum.297
  803.9 19.1 %fusion.51 = (bf16[1024,2048]{1,0:T(8,128)(2,1)}, bf16[1024,2048]{1,0:T(8,128)(2,1)}, bf16[1024,2048]{1,0:T(8,128)(2,1)}) fusion(bf16[1024,2048]{1,0:T(8,128)(2,1)} %reduce_sum.297, f32[2048]{0:T(1024)S(1)} %bitcast.226, bf16[2048,2048]{1,0:T(8,128)(2,1)} %param.14, bf16[1024,2048]{1,0:T(8,128)(2,1)} %reduce_sum.301, f32[1024]{0:T(1024)S(1)} %broadcast_multiply_fusion.4, ...), kind=kLoop, calls=%fused_computation.67 | loop fusion | flops 48234496 | bytes 46186496 | tf_op jit(solution)/shard_map/convert_element_type | solution.py:314
  824.9 2.8 fusion.71
  829.6 4.7 reduce-scatter.7.cloned.1.call-done
  836.2 23.5 %all-reduce.5 = (f32[2,3,256]{2,1,0:T(4,128)S(1)}, f32[2048]{0:T(1024)}) all-reduce(f32[2,3,256]{2,1,0:T(4,128)S(1)} %add.280, f32[2048]{0:T(1024)S(1)} %add.286), channel_id=1, replica_groups=mesh['shard'=8,'tensor'=4] {'shard'}, use_global_device_ids=true, to_apply=%region_37.38 | all-reduce | flops 3584 | bytes 28672 | tf_op jit(solution)/shard_map/psum | solution.py:349
  860.5 19.0 %all-reduce.7 = (bf16[4,2048]{1,0:T(4,128)(2,1)S(1)}, bf16[4,2048]{1,0:T(4,128)(2,1)S(1)}) all-reduce(bf16[4,2048]{1,0:T(4,128)(2,1)S(1)} %pad_maximum_fusion.13, bf16[4,2048]{1,0:T(4,128)(2,1)S(1)} %pad_maximum_fusion.12), channel_id=1, replica_groups=mesh['shard'=8,'tensor'=4] {'tensor'}, use_global_device_ids=true, to_apply=%region_31.32 | all-reduce | flops 16384 | bytes 65536 | tf_op jit(solution)/shard_map/psum | solution.py:332
  879.7 19.7 %reduce-scatter.5.cloned.1.call-done = bf16[256,2,3,256]{3,0,2,1:T(8,128)(2,1)} async-done(((bf16[2048,2,3,256]{3,0,2,1:T(8,128)(2,1)}), bf16[256,2,3,256]{3,0,2,1:T(8,128)(2,1)}) %reduce-scatter.5.cloned.1.call-update) | async-done | bytes 786448 | tf_op jit(solution)/shard_map/reduce_scatter | solution.py:347
  899.3 3.1 copy.155
  902.4 71.9 %reduce-scatter.9.cloned.1.call-done = bf16[256,2048]{1,0:T(8,128)(2,1)} async-done(((bf16[2048,2048]{1,0:T(8,128)(2,1)}), bf16[256,2048]{1,0:T(8,128)(2,1)}) %reduce-scatter.9.cloned.1.call-update) | async-done | bytes 1048592 | tf_op jit(solution)/shard_map/reduce_scatter | solution.py:347
  974.3 2.8 convert_element_type.304
  977.1 71.8 %reduce-scatter.11.cloned.1.call-done = bf16[256,2048]{0,1:T(8,128)(2,1)} async-done(((bf16[2048,2048]{0,1:T(8,128)(2,1)}), bf16[256,2048]{0,1:T(8,128)(2,1)}) %reduce-scatter.11.cloned.1.call-update) | async-done | bytes 1048592 | tf_op jit(solution)/shard_map/reduce_scatter | solution.py:347
  1049.0 2.6 copy.158
  1051.5 8.5 pad_maximum_fusion.1
  1060.0 282.4 %all-reduce.11.cloned.1.call-done = (bf16[1024,2048]{1,0:T(8,128)(2,1)}, bf16[1024,2048]{1,0:T(8,128)(2,1)}) async-done(((bf16[1024,2048]{1,0:T(8,128)(2,1)}, bf16[1024,2048]{1,0:T(8,128)(2,1)}), (bf16[1024,2048]{1,0:T(8,128)(2,1)}, bf16[1024,2048]{1,0:T(8,128)(2,1)})) %all-reduce.11.cloned.1.call-update) | async-done | bytes 8388624 | tf_op jit(solution)/shard_map/psum | solution.py:331
  1342.4 11.3 convert_reduce_fusion.2
  1353.7 23.8 %all-reduce.6 = (bf16[2048]{0:T(1024)(128)(2,1)S(1)}, bf16[2048]{0:T(1024)(128)(2,1)S(1)}, bf16[2048]{0:T(1024)(128)(2,1)S(1)}, bf16[2048]{0:T(1024)(128)(2,1)S(1)}, bf16[2048]{0:T(1024)(128)(2,1)S(1)}) all-reduce(bf16[2048]{0:T(1024)(128)(2,1)S(1)} %get-tuple-element.87, ...), channel_id=4, replica_groups=mesh['shard'=8,'tensor'=4] {'shard'}, use_global_device_ids=true, to_apply=%region_32.33.clone | all-reduce | flops 10240 | bytes 40960
  1380.2 11.8 pad_maximum_fusion
  (286 shorter events, 57.2 us)
Async XLA Ops:
  7.2 5.4 copy-start.64
  7.2 5.4 copy-start.65
  7.2 5.4 copy-start.66
  7.2 5.5 copy-start.67
  7.2 42.0 %copy-start.58 = (bf16[2048]{0:T(1024)(128)(2,1)S(1)}, bf16[2048]{0:T(1024)(128)(2,1)}, u32[]{:S(2)}) copy-start(bf16[2048]{0:T(1024)(128)(2,1)} %param.24) | copy-start | bytes 12292
  7.2 42.0 %copy-start.60 = (bf16[2,3,256]{2,0,1:T(2,128)(2,1)S(1)}, bf16[2,3,256]{2,0,1:T(2,128)(2,1)}, u32[]{:S(2)}) copy-start(bf16[2,3,256]{2,0,1:T(2,128)(2,1)} %param.18) | copy-start | bytes 9220
  7.2 52.0 %all-gather.17.cloned.1.call-start = ((), (), s32[]{:S(2)}) async-start(), calls=%async_computation.5 | async-start | bytes 2359296 | tf_op jit(solution)/shard_map/all_gather | solution.py:299
  9.0 80.0 %all-gather.15.cloned.1.call-start = ((), (), s32[]{:S(2)}) async-start(), calls=%async_computation.4 | async-start | bytes 7077888 | tf_op jit(solution)/shard_map/all_gather | solution.py:298
  11.2 137.4 %all-gather.19.cloned.1.call-start = ((), (), s32[]{:S(2)}) async-start(), calls=%async_computation.6 | async-start | bytes 9437184 | tf_op jit(solution)/shard_map/all_gather | solution.py:300
  11.9 189.3 %all-gather.21.cloned.1.call-start = ((), (), s32[]{:S(2)}) async-start(), calls=%async_computation.7 | async-start | bytes 9437184 | tf_op jit(solution)/shard_map/all_gather | solution.py:301
  12.5 500.8 %all-gather.25.cloned.1.call-start = ((), (), s32[]{:S(2)}) async-start(), calls=%async_computation.13 | async-start | bytes 20971520 | tf_op jit(solution)/shard_map/all_gather | solution.py:13
  23.1 138.3 %copy-start.54 = (f32[8,1,256]{2,1,0:T(1,128)}, f32[8,1,256]{2,1,0:T(1,128)S(1)}, u32[]{:S(2)}) copy-start(f32[8,1,256]{2,1,0:T(1,128)S(1)} %convert_element_type.311) | copy-start | bytes 24580
  32.1 129.3 %copy-start.47 = (f32[8,1,256]{2,1,0:T(1,128)}, f32[8,1,256]{2,1,0:T(1,128)S(1)}, u32[]{:S(2)}) copy-start(f32[8,1,256]{2,1,0:T(1,128)S(1)} %convert_element_type.310) | copy-start | bytes 24580
  40.3 67.9 %copy-start.56 = (f32[8,1,256]{2,1,0:T(1,128)}, f32[8,1,256]{2,1,0:T(1,128)S(1)}, u32[]{:S(2)}) copy-start(f32[8,1,256]{2,1,0:T(1,128)S(1)} %convert_element_type.309) | copy-start | bytes 24580
  49.2 58.9 %copy-start.49 = (f32[8,1,256]{2,1,0:T(1,128)}, f32[8,1,256]{2,1,0:T(1,128)S(1)}, u32[]{:S(2)}) copy-start(f32[8,1,256]{2,1,0:T(1,128)S(1)} %convert_element_type.308) | copy-start | bytes 24580
  49.3 6.6 copy-start
  59.2 77.9 %copy-start.29 = (f32[256,32]{1,0:T(8,128)}, f32[256,32]{1,0:T(8,128)S(1)}, u32[]{:S(2)}) copy-start(f32[256,32]{1,0:T(8,128)S(1)} %get-tuple-element.136) | copy-start | bytes 98308
  59.2 77.9 %copy-start.31 = (f32[256,32]{1,0:T(8,128)}, f32[256,32]{1,0:T(8,128)S(1)}, u32[]{:S(2)}) copy-start(f32[256,32]{1,0:T(8,128)S(1)} %get-tuple-element.137) | copy-start | bytes 98308
  64.5 58.9 %copy-start.24 = (bf16[1024,2,256]{2,0,1:T(8,128)(2,1)}, bf16[1024,2,256]{2,0,1:T(8,128)(2,1)S(1)}, u32[]{:S(2)}) copy-start(bf16[1024,2,256]{2,0,1:T(8,128)(2,1)S(1)} %fusion.134) | copy-start | bytes 3145732
  100.5 7.7 slice-start
  100.5 7.7 slice-start.6
  103.7 6.2 slice-start.1
  103.7 6.8 slice-start.7
  117.3 6.1 copy-start.6
  118.9 4.0 copy-start.38
  119.7 3.6 copy-start.43
  123.0 8.3 copy-start.1
  125.2 6.1 copy-start.37
  137.1 7.0 copy-start.33
  137.1 7.0 copy-start.35
  148.6 16.0 %copy-start.61 = (bf16[2048,2048]{1,0:T(8,128)(2,1)S(1)}, bf16[2048,2048]{1,0:T(8,128)(2,1)}, u32[]{:S(2)}) copy-start(bf16[2048,2048]{1,0:T(8,128)(2,1)} %all-gather.19.cloned.1.call-done) | copy-start | bytes 25165828
  201.2 12.7 copy-start.62
  218.4 573.3 %all-gather.23.cloned.1.call-start = ((), (), s32[]{:S(2)}) async-start(), calls=%async_computation.12 | async-start | bytes 20971520 | tf_op jit(solution)/shard_map/all_gather | solution.py:13
  221.5 11.8 copy-start.27
  221.9 11.4 copy-start.63
  237.7 596.6 %reduce-scatter.7.cloned.1.call-start = ((), (), s32[]{:S(2)}) async-start(), calls=%async_computation.9 | async-start | bytes 2359296 | tf_op jit(solution)/shard_map/reduce_scatter | solution.py:347
  238.2 5.3 copy-start.8
  243.6 10.1 copy-start.26
  265.8 4.7 copy-start.28
  270.6 6.4 copy-start.50
  270.6 6.4 copy-start.57
  276.9 622.5 %reduce-scatter.5.cloned.1.call-start = ((), (), s32[]{:S(2)}) async-start(), calls=%async_computation.8 | async-start | bytes 7077888 | tf_op jit(solution)/shard_map/reduce_scatter | solution.py:347
  276.9 14.8 %copy-start.34 = (bf16[4,256,2,192]{3,1,2,0:T(8,128)(2,1)S(1)}, bf16[4,256,2,192]{3,1,2,0:T(8,128)(2,1)}, u32[]{:S(2)}) copy-start(bf16[4,256,2,192]{3,1,2,0:T(8,128)(2,1)} %slice.350) | copy-start | bytes 2359300
  299.7 4.9 copy-start.12
  304.5 15.3 %copy-start.16 = (f32[4,256,2,256]{3,1,0,2:T(8,128)}, f32[4,256,2,256]{3,1,0,2:T(8,128)S(1)}, u32[]{:S(2)}) copy-start(f32[4,256,2,256]{3,1,0,2:T(8,128)S(1)} %copy.141) | copy-start | bytes 6291460
  319.9 654.5 %reduce-scatter.9.cloned.1.call-start = ((), (), s32[]{:S(2)}) async-start(), calls=%async_computation.10 | async-start | bytes 9437184 | tf_op jit(solution)/shard_map/reduce_scatter | solution.py:347
  319.9 18.8 %copy-start.48 = (f32[8,1,256]{2,1,0:T(1,128)S(1)}, f32[8,1,256]{2,1,0:T(1,128)}, u32[]{:S(2)}) copy-start(f32[8,1,256]{2,1,0:T(1,128)} %copy-done.47) | copy-start | bytes 24580
  319.9 18.8 %copy-start.55 = (f32[8,1,256]{2,1,0:T(1,128)S(1)}, f32[8,1,256]{2,1,0:T(1,128)}, u32[]{:S(2)}) copy-start(f32[8,1,256]{2,1,0:T(1,128)} %copy-done.54) | copy-start | bytes 24580
  338.7 33.8 %slice-start.2 = ((s8[8388608]{0:T(1024)(128)(4,1)}), s8[4194304]{0:T(1024)(128)(4,1)S(1)}, s32[]{:S(2)}) async-start(s8[8388608]{0:T(1024)(128)(4,1)} %bitcast.168), calls=%async_computation.17 | async-start | bytes 8388608
  353.8 18.7 %slice-start.3 = ((s8[8388608]{0:T(1024)(128)(4,1)}), s8[4194304]{0:T(1024)(128)(4,1)S(1)}, s32[]{:S(2)}) async-start(s8[8388608]{0:T(1024)(128)(4,1)} %bitcast.168), calls=%async_computation.18 | async-start | bytes 8388608
  389.3 659.7 %reduce-scatter.11.cloned.1.call-start = ((), (), s32[]{:S(2)}) async-start(), calls=%async_computation.11 | async-start | bytes 9437184 | tf_op jit(solution)/shard_map/reduce_scatter | solution.py:347
  407.0 15.7 %copy-start.71 = (bf16[1024,2048]{1,0:T(8,128)(2,1)S(1)}, bf16[1024,2048]{1,0:T(8,128)(2,1)}, u32[]{:S(2)}) copy-start(bf16[1024,2048]{1,0:T(8,128)(2,1)} %get-tuple-element.135) | copy-start | bytes 12582916
  438.5 13.1 copy-start.9
  438.6 903.9 %all-reduce.11.cloned.1.call-start = ((), (), s32[]{:S(2)}) async-start(), calls=%async_computation.14 | async-start | bytes 16777216 | tf_op jit(solution)/shard_map/psum | solution.py:331
  438.6 13.1 copy-start.10
  438.6 13.1 copy-start.11
  438.6 24.1 %slice-start.4 = ((s8[8388608]{0:T(1024)(128)(4,1)}), s8[4194304]{0:T(1024)(128)(4,1)S(1)}, s32[]{:S(2)}) async-start(s8[8388608]{0:T(1024)(128)(4,1)} %bitcast.239), calls=%async_computation.19 | async-start | bytes 8388608
  451.7 11.0 slice-start.5
  451.7 11.0 copy-start.75
  462.7 11.1 copy-start.51
  824.9 4.3 copy-start.17
  829.2 7.0 copy-start.52
  829.2 7.0 copy-start.53
  1378.3 13.8 copy-start.59
  (31 other events, 72.1 us)
Sparse Core Ops, SparseCore 0:
  10.5 30.5 all-gather.16
  43.6 45.3 all-gather.14
  90.9 54.2 all-gather.18
  146.9 54.2 all-gather.20
  218.5 286.7 all-gather.24
  506.7 284.9 all-gather.22
  795.0 39.2 reduce-scatter.6
  837.7 61.6 reduce-scatter.4
  902.8 71.4 reduce-scatter.8
  977.6 71.2 reduce-scatter.10
  1051.6 290.8 all-reduce.10
